TPU v7x, 32 devices: a whole 2x2x4 slice. The times are simulated.
32 devices in a mesh: pq: 8 (over z, x), hh: 4 (over y, core).
Axes of the slice: x: 2, y: 2, z: 4, core: 2. Of those that a mesh axis runs over, the one named last changes fastest.
Arguments:
- amplitudes: bfloat16 [4096, 2048], P('hh', 'pq'), may hold values from -6 to 6
- integrals: bfloat16 [4096, 2048], P('hh', 'pq'), may hold values from -0.001953125 to 0.001953125
- left_amps: bfloat16 [8, 4096, 1024], P(None, 'hh', 'pq'), may hold values from -6 to 6
Outputs:
- sigma_ladder: bfloat16 [8, 4096, 1024], P(None, 'hh', 'pq')
- subspace: float32 [8, 8], replicated
All inputs are finite; a program needn't handle non-finite values.
Results may differ from a plain program's by a relative error of at most 0.0049.
Values may be sent and summed in bfloat16 or wider, within the bound.
No kernel may reach another device: no remote copies, remote signals or barrier semaphores. Data moves between devices by JAX's collectives and lax.ppermute only.
A program may use at most 64 MiB of HBM per device.

v0:
```python
import math
import jax
import jax.numpy as jnp
from jax import lax
from jax.sharding import PartitionSpec as P

OCC_PAIRS = 4096


def body(amplitudes, integrals, left_amps):
    root_count = left_amps.shape[0]
    ab_cols = left_amps.shape[2]
    partial_t = lax.dot_general(
        integrals,
        lax.all_gather(amplitudes, "hh", axis=0, tiled=True),
        (((1,), (1,)), ((), ())),
        preferred_element_type=jnp.float32,
    )
    ladder_t = lax.psum_scatter(partial_t, "pq", scatter_dimension=1, tiled=True).astype(
        jnp.bfloat16
    )
    ladder_t = lax.all_gather(ladder_t, "pq", axis=1, tiled=True)
    rows_out = lax.dot_general(
        ladder_t,
        lax.all_gather(left_amps, "hh", axis=1, tiled=True),
        (((1,), (1,)), ((), ())),
        preferred_element_type=jnp.float32,
    )
    sigma_out = jnp.transpose(rows_out, (1, 0, 2)).astype(jnp.bfloat16)
    local_gram = jnp.dot(
        left_amps.reshape(root_count, -1),
        sigma_out.reshape(root_count, -1).T,
        preferred_element_type=jnp.float32,
    )
    factor = 1.0 / math.sqrt(OCC_PAIRS * ab_cols * lax.axis_size("pq"))
    subspace = lax.psum(local_gram, ("pq", "hh")) * factor
    return (sigma_out, subspace)


def solution(mesh):
    return jax.shard_map(
        body,
        mesh=mesh,
        in_specs=(P("hh", "pq"), P("hh", "pq"), P(None, "hh", "pq")),
        out_specs=(P(None, "hh", "pq"), P()),
        check_vma=False,
    )
```

profile of v0, /device:TPU:10, one launch (start us, length us, event | category | flops | bytes accessed | tf_op | source)
XLA Modules:
  0.0 574.5 jit_solution(7617182189609885000)
XLA Ops:
  7.2 0.0 copy-start
  7.2 0.0 all-gather.4.cloned.1.call-start
  7.2 0.7 all-gather.4.cloned.1.call-update
  7.9 0.0 reduce-scatter.2.cloned.1.call-start
  8.0 25.3 %all-gather.4.cloned.1.call-done = bf16[4096,256]{1,0:T(8,128)(2,1)} async-done(((bf16[1024,256]{1,0:T(8,128)(2,1)}), bf16[4096,256]{1,0:T(8,128)(2,1)}) %all-gather.4.cloned.1.call-update) | async-done | bytes 2097168 | tf_op jit(solution)/shard_map/all_gather | solution.py:15
  33.3 0.0 copy-done
  33.3 9.7 %fusion.12 = f32[1024,4096]{1,0:T(8,128)} fusion(bf16[1024,256]{1,0:T(8,128)(2,1)S(1)} %copy-done, bf16[4096,256]{1,0:T(8,128)(2,1)} %all-gather.4.cloned.1.call-done), kind=kOutput, calls=%fused_computation.8 | convolution fusion | flops 2147483648 | bytes 19398656 | tf_op jit(solution)/shard_map/dot_general | solution.py:13
  43.0 0.0 reduce-scatter.2.cloned.1.call-update
  43.0 0.0 all-gather.8.cloned.1.call-start
  43.1 0.7 all-gather.8.cloned.1.call-update
  43.7 0.0 all-gather.6.cloned.1.call-start
  43.8 278.5 %reduce-scatter.2.cloned.1.call-done = f32[1024,512]{1,0:T(8,128)} async-done(((f32[1024,4096]{1,0:T(8,128)}), f32[1024,512]{1,0:T(8,128)}) %reduce-scatter.2.cloned.1.call-update) | async-done | bytes 2097168 | tf_op jit(solution)/shard_map/reduce_scatter | solution.py:19
  322.3 2.7 convert_element_type.9
  325.0 0.0 all-gather.6.cloned.1.call-update
  325.1 0.0 copy-start.1
  325.1 57.3 %all-gather.8.cloned.1.call-done = bf16[8,4096,128]{2,1,0:T(8,128)(2,1)} async-done(((bf16[8,1024,128]{2,1,0:T(8,128)(2,1)}), bf16[8,4096,128]{2,1,0:T(8,128)(2,1)}) %all-gather.8.cloned.1.call-update) | async-done | bytes 8388624 | tf_op jit(solution)/shard_map/all_gather | solution.py:25
  382.3 124.7 %all-gather.6.cloned.1.call-done = bf16[1024,4096]{1,0:T(8,128)(2,1)} async-done(((bf16[1024,512]{1,0:T(8,128)(2,1)}), bf16[1024,4096]{1,0:T(8,128)(2,1)}) %all-gather.6.cloned.1.call-update) | async-done | bytes 8388624 | tf_op jit(solution)/shard_map/all_gather | solution.py:22
  507.0 13.7 %convert_bitcast_fusion = bf16[8,1024,128]{2,1,0:T(8,128)(2,1)S(1)} fusion(bf16[8,4096,128]{2,1,0:T(8,128)(2,1)} %all-gather.8.cloned.1.call-done, bf16[1024,4096]{1,0:T(8,128)(2,1)} %all-gather.6.cloned.1.call-done), kind=kOutput, calls=%fused_computation.5 | convolution fusion | flops 8590983168 | bytes 18874368 | tf_op jit(solution)/shard_map/dot_general | solution.py:23
  520.7 0.0 copy-start.2
  520.7 1.3 copy-done.2
  522.0 0.0 copy-done.1
  522.0 2.5 fusion.7
  524.5 42.8 %psum.7 = f32[8,8]{0,1:T(8,128)S(1)} all-reduce(f32[8,8]{0,1:T(8,128)S(1)} %fusion.7), channel_id=1, replica_groups=mesh['pq'=8,'hh'=4] {'pq','hh'}, use_global_device_ids=true, to_apply=%region_1.0 | all-reduce | flops 64 | bytes 512 | tf_op jit(solution)/shard_map/psum | solution.py:36
  567.3 0.7 copy.7
  (1 shorter events, 0.0 us)
Async XLA Ops:
  7.2 26.1 %copy-start = (bf16[1024,256]{1,0:T(8,128)(2,1)S(1)}, bf16[1024,256]{1,0:T(8,128)(2,1)}, u32[]{:S(2)}) copy-start(bf16[1024,256]{1,0:T(8,128)(2,1)} %param.4) | copy-start | bytes 1572868
  7.2 26.1 %all-gather.4.cloned.1.call-start = ((), (), s32[]{:S(2)}) async-start(), calls=%async_computation.1 | async-start | bytes 2621440 | tf_op jit(solution)/shard_map/all_gather | solution.py:15
  7.9 314.4 %reduce-scatter.2.cloned.1.call-start = ((), (), s32[]{:S(2)}) async-start(), calls=%async_computation.2 | async-start | bytes 18874368 | tf_op jit(solution)/shard_map/reduce_scatter | solution.py:19
  43.0 339.3 %all-gather.8.cloned.1.call-start = ((), (), s32[]{:S(2)}) async-start(), calls=%async_computation.4 | async-start | bytes 10485760 | tf_op jit(solution)/shard_map/all_gather | solution.py:25
  43.7 463.3 %all-gather.6.cloned.1.call-start = ((), (), s32[]{:S(2)}) async-start(), calls=%async_computation.3 | async-start | bytes 9437184 | tf_op jit(solution)/shard_map/all_gather | solution.py:22
  325.1 196.9 %copy-start.1 = (bf16[8,1024,128]{2,1,0:T(8,128)(2,1)S(1)}, bf16[8,1024,128]{2,1,0:T(8,128)(2,1)}, u32[]{:S(2)}) copy-start(bf16[8,1024,128]{2,1,0:T(8,128)(2,1)} %param.5) | copy-start | bytes 6291460
  520.7 1.3 copy-start.2
Sparse Core Ops, SparseCore 0:
  9.5 23.6 all-gather.3
  43.1 279.1 reduce-scatter.1
  323.9 58.3 all-gather.7
  384.8 122.1 all-gather.5
where the time goes:
time: 575 us; the launch traced here: 574 us
  waiting for transfers between devices  487 us (85%)
  blocking collectives  42.8 us (7%)
  matrix products  25.9 us (5%)
  between operations  13.8 us (2%)
    reduce_scatter x1, waiting for transfers between devices, body(): lax.psum_scatter(partial_t, 'pq', scatter_dimension=1, tiled=True)  279 us
    all_gather x1, waiting for transfers between devices, body(): ladder_t = lax.all_gather(ladder_t, 'pq', axis=1, tiled=True)  125 us
    all_gather x1, waiting for transfers between devices, body(): lax.all_gather(left_amps, 'hh', axis=1, tiled=True)  57.3 us
    psum x1, blocking collectives, body(): subspace = lax.psum(local_gram, ('pq', 'hh')) * factor  42.8 us
    all_gather x1, waiting for transfers between devices, body(): lax.all_gather(amplitudes, 'hh', axis=0, tiled=True)  25.3 us
    dot_general x1, matrix products, body(): lax.dot_general(ladder_t, lax.all_gather(left_amps, 'hh', axis=1, tiled=T...  13.7 us
  transfers between devices with their start and end apart: 4, of which 4 were waited for; matrix products, arithmetic and copies ran while one was open for 0% of the time, Pallas kernels for 0%

commit v1 on v0

--- a/solution.py
+++ b/solution.py
@@ -5,6 +5,11 @@
 from jax.sharding import PartitionSpec as P
 
 OCC_PAIRS = 4096
+
+
+def by_each_axis(array, axis_one, axis_two):
+    half = lax.psum(array, axis_one)
+    return lax.psum(half, axis_two)
 
 
 def body(amplitudes, integrals, left_amps):
@@ -33,7 +38,7 @@
         preferred_element_type=jnp.float32,
     )
     factor = 1.0 / math.sqrt(OCC_PAIRS * ab_cols * lax.axis_size("pq"))
-    subspace = lax.psum(local_gram, ("pq", "hh")) * factor
+    subspace = by_each_axis(local_gram, "hh", "pq") * factor
     return (sigma_out, subspace)
 
 

time: 575 us -> 562 us (0.977); the launches traced: 574 us -> 555 us
  blocking collectives: 42.8 us -> 23.6 us
    psum x1 -> x2, blocking collectives: 42.8 us -> 23.6 us  [the longest x1 17.8 us: by_each_axis(): return lax.psum(half, axis_two)]
where the time goes in v1:
time: 562 us; the launch traced here: 555 us
  waiting for transfers between devices  487 us (87%)
  matrix products  25.9 us (5%)
  blocking collectives  23.6 us (4%)
  between operations  13.8 us (2%)
    reduce_scatter x1, waiting for transfers between devices, body(): lax.psum_scatter(partial_t, 'pq', scatter_dimension=1, tiled=True)  279 us
    all_gather x1, waiting for transfers between devices, body(): ladder_t = lax.all_gather(ladder_t, 'pq', axis=1, tiled=True)  125 us
    all_gather x1, waiting for transfers between devices, body(): lax.all_gather(left_amps, 'hh', axis=1, tiled=True)  57.3 us
    all_gather x1, waiting for transfers between devices, body(): lax.all_gather(amplitudes, 'hh', axis=0, tiled=True)  25.3 us
    psum x1, blocking collectives, by_each_axis(): return lax.psum(half, axis_two)  17.8 us
    dot_general x1, matrix products, body(): lax.dot_general(ladder_t, lax.all_gather(left_amps, 'hh', axis=1, tiled=T...  13.7 us
  transfers between devices with their start and end apart: 4, of which 4 were waited for; matrix products, arithmetic and copies ran while one was open for 0% of the time, Pallas kernels for 0%

profile of v1, /device:TPU:10, one launch (start us, length us, event | category | flops | bytes accessed | tf_op | source)
XLA Modules:
  0.0 555.3 jit_solution(4055228888567046507)
XLA Ops:
  7.2 0.0 copy-start
  7.2 0.0 all-gather.4.cloned.1.call-start
  7.2 0.7 all-gather.4.cloned.1.call-update
  7.9 0.0 reduce-scatter.2.cloned.1.call-start
  8.0 25.3 %all-gather.4.cloned.1.call-done = bf16[4096,256]{1,0:T(8,128)(2,1)} async-done(((bf16[1024,256]{1,0:T(8,128)(2,1)}), bf16[4096,256]{1,0:T(8,128)(2,1)}) %all-gather.4.cloned.1.call-update) | async-done | bytes 2097168 | tf_op jit(solution)/shard_map/all_gather | solution.py:20
  33.3 0.0 copy-done
  33.3 9.7 %fusion.12 = f32[1024,4096]{1,0:T(8,128)} fusion(bf16[1024,256]{1,0:T(8,128)(2,1)S(1)} %copy-done, bf16[4096,256]{1,0:T(8,128)(2,1)} %all-gather.4.cloned.1.call-done), kind=kOutput, calls=%fused_computation.8 | convolution fusion | flops 2147483648 | bytes 19398656 | tf_op jit(solution)/shard_map/dot_general | solution.py:18
  43.0 0.0 reduce-scatter.2.cloned.1.call-update
  43.0 0.0 all-gather.8.cloned.1.call-start
  43.1 0.7 all-gather.8.cloned.1.call-update
  43.7 0.0 all-gather.6.cloned.1.call-start
  43.8 278.5 %reduce-scatter.2.cloned.1.call-done = f32[1024,512]{1,0:T(8,128)} async-done(((f32[1024,4096]{1,0:T(8,128)}), f32[1024,512]{1,0:T(8,128)}) %reduce-scatter.2.cloned.1.call-update) | async-done | bytes 2097168 | tf_op jit(solution)/shard_map/reduce_scatter | solution.py:24
  322.3 2.7 convert_element_type.9
  325.0 0.0 all-gather.6.cloned.1.call-update
  325.1 0.0 copy-start.1
  325.1 57.3 %all-gather.8.cloned.1.call-done = bf16[8,4096,128]{2,1,0:T(8,128)(2,1)} async-done(((bf16[8,1024,128]{2,1,0:T(8,128)(2,1)}), bf16[8,4096,128]{2,1,0:T(8,128)(2,1)}) %all-gather.8.cloned.1.call-update) | async-done | bytes 8388624 | tf_op jit(solution)/shard_map/all_gather | solution.py:30
  382.3 124.7 %all-gather.6.cloned.1.call-done = bf16[1024,4096]{1,0:T(8,128)(2,1)} async-done(((bf16[1024,512]{1,0:T(8,128)(2,1)}), bf16[1024,4096]{1,0:T(8,128)(2,1)}) %all-gather.6.cloned.1.call-update) | async-done | bytes 8388624 | tf_op jit(solution)/shard_map/all_gather | solution.py:27
  507.0 13.7 %convert_bitcast_fusion = bf16[8,1024,128]{2,1,0:T(8,128)(2,1)S(1)} fusion(bf16[8,4096,128]{2,1,0:T(8,128)(2,1)} %all-gather.8.cloned.1.call-done, bf16[1024,4096]{1,0:T(8,128)(2,1)} %all-gather.6.cloned.1.call-done), kind=kOutput, calls=%fused_computation.5 | convolution fusion | flops 8590983168 | bytes 18874368 | tf_op jit(solution)/shard_map/dot_general | solution.py:28
  520.7 0.0 copy-start.2
  520.7 1.3 copy-done.2
  522.0 0.0 copy-done.1
  522.0 2.5 fusion.7
  524.5 5.8 %psum.14 = f32[8,8]{0,1:T(8,128)S(1)} all-reduce(f32[8,8]{0,1:T(8,128)S(1)} %fusion.7), channel_id=1, replica_groups=mesh['pq'=8,'hh'=4] {'hh'}, use_global_device_ids=true, to_apply=%region_1.0 | all-reduce | flops 64 | bytes 512 | tf_op jit(solution)/shard_map/psum | solution.py:11
  530.4 17.8 %psum.15 = f32[8,8]{0,1:T(8,128)S(1)} all-reduce(f32[8,8]{0,1:T(8,128)S(1)} %psum.14), channel_id=1, replica_groups=mesh['pq'=8,'hh'=4] {'pq'}, use_global_device_ids=true, to_apply=%region_2.0 | all-reduce | flops 64 | bytes 512 | tf_op jit(solution)/shard_map/psum | solution.py:12
  548.1 0.7 copy.7
  (1 shorter events, 0.0 us)
Async XLA Ops:
  7.2 26.1 %copy-start = (bf16[1024,256]{1,0:T(8,128)(2,1)S(1)}, bf16[1024,256]{1,0:T(8,128)(2,1)}, u32[]{:S(2)}) copy-start(bf16[1024,256]{1,0:T(8,128)(2,1)} %param.4) | copy-start | bytes 1572868
  7.2 26.1 %all-gather.4.cloned.1.call-start = ((), (), s32[]{:S(2)}) async-start(), calls=%async_computation.1 | async-start | bytes 2621440 | tf_op jit(solution)/shard_map/all_gather | solution.py:20
  7.9 314.4 %reduce-scatter.2.cloned.1.call-start = ((), (), s32[]{:S(2)}) async-start(), calls=%async_computation.2 | async-start | bytes 18874368 | tf_op jit(solution)/shard_map/reduce_scatter | solution.py:24
  43.0 339.3 %all-gather.8.cloned.1.call-start = ((), (), s32[]{:S(2)}) async-start(), calls=%async_computation.4 | async-start | bytes 10485760 | tf_op jit(solution)/shard_map/all_gather | solution.py:30
  43.7 463.3 %all-gather.6.cloned.1.call-start = ((), (), s32[]{:S(2)}) async-start(), calls=%async_computation.3 | async-start | bytes 9437184 | tf_op jit(solution)/shard_map/all_gather | solution.py:27
  325.1 196.9 %copy-start.1 = (bf16[8,1024,128]{2,1,0:T(8,128)(2,1)S(1)}, bf16[8,1024,128]{2,1,0:T(8,128)(2,1)}, u32[]{:S(2)}) copy-start(bf16[8,1024,128]{2,1,0:T(8,128)(2,1)} %param.5) | copy-start | bytes 6291460
  520.7 1.3 copy-start.2
Sparse Core Ops, SparseCore 0:
  9.5 23.6 all-gather.3
  43.1 279.1 reduce-scatter.1
  323.9 58.3 all-gather.7
  384.8 122.1 all-gather.5

commit v2 on v0

--- a/solution.py
+++ b/solution.py
@@ -5,6 +5,13 @@
 from jax.sharding import PartitionSpec as P
 
 OCC_PAIRS = 4096
+
+
+def swapped_in(array, name, d):
+    peers = lax.axis_size(name)
+    parts = jnp.stack([array for _ in range(peers)])
+    parts = lax.all_to_all(parts, name, split_axis=0, concat_axis=0)
+    return jnp.concatenate(parts, axis=d)
 
 
 def body(amplitudes, integrals, left_amps):
@@ -22,7 +29,7 @@
     ladder_t = lax.all_gather(ladder_t, "pq", axis=1, tiled=True)
     rows_out = lax.dot_general(
         ladder_t,
-        lax.all_gather(left_amps, "hh", axis=1, tiled=True),
+        swapped_in(left_amps, "hh", 1),
         (((1,), (1,)), ((), ())),
         preferred_element_type=jnp.float32,
     )

time: 575 us -> 515 us (0.90)
  waiting for transfers between devices: 487 us -> 321 us
  blocking collectives: 42.8 us -> 140 us
  local copies, waits for them, and re-layouts: 1.99 us -> 11.5 us
    all_gather x1, waiting for transfers between devices: 125 us -> 16 us  [body(): ladder_t = lax.all_gather(ladder_t, 'pq', axis=1, tiled=True)]
    all_to_all x0 -> x1, blocking collectives: none -> 96.9 us  [swapped_in(): parts = lax.all_to_all(parts, name, split_axis=0, concat_axis=0)]
    all_gather x1 -> x0, waiting for transfers between devices: 57.3 us -> none  [body(): lax.all_gather(left_amps, 'hh', axis=1, tiled=True)]
    reshape x0 -> x1, local copies, waits for them, and re-layouts: none -> 7.67 us  [swapped_in(): return jnp.concatenate(parts, axis=d)]
  transfers between devices with their start and end apart: 4 -> 3, of which waited for: 4 -> 3; matrix products, arithmetic and copies ran while one was open for 0% -> 2% of each run, Pallas kernels for 0% -> 0%
where the time goes in v2:
time: 515 us
  waiting for transfers between devices  321 us (62%)
  blocking collectives  140 us (27%)
  matrix products  25.9 us (5%)
  between operations  13.8 us (3%)
  local copies, waits for them, and re-layouts  11.5 us (2%)
    reduce_scatter x1, waiting for transfers between devices, body(): lax.psum_scatter(partial_t, 'pq', scatter_dimension=1, tiled=True)  279 us
    all_to_all x1, blocking collectives, swapped_in(): parts = lax.all_to_all(parts, name, split_axis=0, concat_axis=0)  96.9 us
    psum x1, blocking collectives, body(): subspace = lax.psum(local_gram, ('pq', 'hh')) * factor  42.7 us
    all_gather x1, waiting for transfers between devices, body(): lax.all_gather(amplitudes, 'hh', axis=0, tiled=True)  25.3 us
    all_gather x1, waiting for transfers between devices, body(): ladder_t = lax.all_gather(ladder_t, 'pq', axis=1, tiled=True)  16 us
    dot_general x1, matrix products, body(): lax.dot_general(ladder_t, swapped_in(left_amps, 'hh', 1), (((1,), (1,)),...  13.7 us
  transfers between devices with their start and end apart: 3, of which 3 were waited for; matrix products, arithmetic and copies ran while one was open for 2% of the time, Pallas kernels for 0%

profile of v2, /device:TPU:10, one launch (start us, length us, event | category | flops | bytes accessed | tf_op | source)
XLA Modules:
  0.0 515.0 jit_solution(2135595707194265119)
XLA Ops:
  7.2 0.0 copy-start
  7.2 0.0 all-gather.3.cloned.1.call-start
  7.2 0.7 all-gather.3.cloned.1.call-update
  7.9 0.0 reduce-scatter.2.cloned.1.call-start
  8.0 25.3 %all-gather.3.cloned.1.call-done = bf16[4096,256]{1,0:T(8,128)(2,1)} async-done(((bf16[1024,256]{1,0:T(8,128)(2,1)}), bf16[4096,256]{1,0:T(8,128)(2,1)}) %all-gather.3.cloned.1.call-update) | async-done | bytes 2097168 | tf_op jit(solution)/shard_map/all_gather | solution.py:22
  33.3 0.0 copy-done
  33.3 9.7 %fusion.12 = f32[1024,4096]{1,0:T(8,128)} fusion(bf16[1024,256]{1,0:T(8,128)(2,1)S(1)} %copy-done, bf16[4096,256]{1,0:T(8,128)(2,1)} %all-gather.3.cloned.1.call-done), kind=kOutput, calls=%fused_computation.8 | convolution fusion | flops 2147483648 | bytes 19398656 | tf_op jit(solution)/shard_map/dot_general | solution.py:20
  43.0 0.0 reduce-scatter.2.cloned.1.call-update
  43.0 0.0 copy-start.1
  43.0 0.0 all-gather.5.cloned.1.call-start
  43.1 279.3 %reduce-scatter.2.cloned.1.call-done = f32[1024,512]{1,0:T(8,128)} async-done(((f32[1024,4096]{1,0:T(8,128)}), f32[1024,512]{1,0:T(8,128)}) %reduce-scatter.2.cloned.1.call-update) | async-done | bytes 2097168 | tf_op jit(solution)/shard_map/reduce_scatter | solution.py:26
  322.3 2.7 convert_element_type.9
  325.0 0.0 all-gather.5.cloned.1.call-update
  325.1 0.0 copy-done.1
  325.1 1.9 stack.2
  326.9 96.9 %all_to_all.5 = bf16[4,8,1024,128]{3,2,1,0:T(8,128)(2,1)} all-to-all(bf16[4,8,1024,128]{3,2,1,0:T(8,128)(2,1)S(1)} %stack.2), channel_id=1, replica_groups=mesh['pq'=8,'hh'=4] {'hh'}, dimensions={0} | all-to-all | bytes 16777216 | tf_op jit(solution)/shard_map/all_to_all | solution.py:13
  423.8 7.7 %copy.8 = bf16[8,4,1024,128]{3,2,1,0:T(8,128)(2,1)} copy(bf16[8,4,1024,128]{3,2,0,1:T(8,128)(2,1)} %bitcast.16) | data formatting | bytes 16777216 | tf_op jit(solution)/shard_map/reshape | solution.py:14
  431.5 16.0 %all-gather.5.cloned.1.call-done = bf16[1024,4096]{1,0:T(8,128)(2,1)} async-done(((bf16[1024,512]{1,0:T(8,128)(2,1)}), bf16[1024,4096]{1,0:T(8,128)(2,1)}) %all-gather.5.cloned.1.call-update) | async-done | bytes 8388624 | tf_op jit(solution)/shard_map/all_gather | solution.py:29
  447.5 13.7 %convert_bitcast_fusion = bf16[8,1024,128]{2,1,0:T(8,128)(2,1)S(1)} fusion(bf16[8,4096,128]{2,1,0:T(8,128)(2,1)} %bitcast.17, bf16[1024,4096]{1,0:T(8,128)(2,1)} %all-gather.5.cloned.1.call-done), kind=kOutput, calls=%fused_computation.5 | convolution fusion | flops 8590983168 | bytes 18874368 | tf_op jit(solution)/shard_map/dot_general | solution.py:30
  461.2 0.0 copy-start.2
  461.2 1.3 copy-done.2
  462.5 2.5 fusion.7
  465.0 42.7 %psum.7 = f32[8,8]{0,1:T(8,128)S(1)} all-reduce(f32[8,8]{0,1:T(8,128)S(1)} %fusion.7), channel_id=1, replica_groups=mesh['pq'=8,'hh'=4] {'pq','hh'}, use_global_device_ids=true, to_apply=%region_1.0 | all-reduce | flops 64 | bytes 512 | tf_op jit(solution)/shard_map/psum | solution.py:43
  507.8 0.7 copy.11
  (1 shorter events, 0.0 us)
Async XLA Ops:
  7.2 26.1 %copy-start = (bf16[1024,256]{1,0:T(8,128)(2,1)S(1)}, bf16[1024,256]{1,0:T(8,128)(2,1)}, u32[]{:S(2)}) copy-start(bf16[1024,256]{1,0:T(8,128)(2,1)} %param.4) | copy-start | bytes 1572868
  7.2 26.1 %all-gather.3.cloned.1.call-start = ((), (), s32[]{:S(2)}) async-start(), calls=%async_computation.2 | async-start | bytes 2621440 | tf_op jit(solution)/shard_map/all_gather | solution.py:22
  7.9 314.4 %reduce-scatter.2.cloned.1.call-start = ((), (), s32[]{:S(2)}) async-start(), calls=%async_computation.3 | async-start | bytes 18874368 | tf_op jit(solution)/shard_map/reduce_scatter | solution.py:26
  43.0 282.0 %copy-start.1 = (bf16[8,1024,128]{2,1,0:T(8,128)(2,1)S(1)}, bf16[8,1024,128]{2,1,0:T(8,128)(2,1)}, u32[]{:S(2)}) copy-start(bf16[8,1024,128]{2,1,0:T(8,128)(2,1)} %param.5) | copy-start | bytes 6291460
  43.0 404.5 %all-gather.5.cloned.1.call-start = ((), (), s32[]{:S(2)}) async-start(), calls=%async_computation.4 | async-start | bytes 9437184 | tf_op jit(solution)/shard_map/all_gather | solution.py:29
  461.2 1.3 copy-start.2
Sparse Core Ops, SparseCore 0:
  9.5 23.6 all-gather.2
  43.1 279.1 reduce-scatter.1
  325.2 122.2 all-gather.4
